TPU v7x, 32 devices: a whole 2x2x4 slice. The times are simulated.
32 devices in a mesh: ia: 4 (over y, x), ja: 4 (over z), col: 2 (over core).
Axes of the slice: x: 2, y: 2, z: 4, core: 2. Of those that a mesh axis runs over, the one named last changes fastest.
Arguments:
- pair_rep: bfloat16 [512, 512, 128], P('ia', 'ja'), may hold values from -6 to 6
- norm_gain: float32 [128], replicated, may hold values from 0.1 to 1.9
- weights: bfloat16 [4, 128, 128], P(None, None, 'col'), may hold values from -0.5 to 0.5
- residue_mask: int32 [512], replicated, may hold values 0 or 1
- product_grad: bfloat16 [512, 128, 512], P('ia', 'col', 'ja'), may hold values from -1 to 1
Outputs:
- pair_grad: bfloat16 [512, 512, 128], P('ia', 'ja')
- weight_grads: float32 [4, 128, 128], P(None, None, 'col')
All inputs are finite; a program needn't handle non-finite values.
Results may differ from a plain program's by a relative error of at most 0.0067.
Values may be sent and summed in bfloat16 or wider, within the bound.
A program may use at most 128 MiB of HBM per device.

v0:
```python
import jax
import jax.numpy as jnp
from jax import lax
from jax.sharding import PartitionSpec as P

CLIP_LIMIT = 64.0


def gate_terms(incoming, linear, gate_pre, pair_valid):
    sigmoid_gate = jax.nn.sigmoid(gate_pre)
    through = incoming * pair_valid
    return (through * sigmoid_gate, through * linear * sigmoid_gate * (1.0 - sigmoid_gate))


def on_device(pair_rep, norm_gain, weights, residue_mask, product_grad):
    row_count = pair_rep.shape[0]
    col_count = pair_rep.shape[1]
    row_first = lax.axis_index("ia") * row_count
    col_first = lax.axis_index("ja") * col_count
    validity = residue_mask.astype(jnp.float32)
    row_valid = lax.dynamic_slice_in_dim(validity, row_first, row_count)
    col_valid = lax.dynamic_slice_in_dim(validity, col_first, col_count)
    pair_valid = row_valid[:, None, None] * col_valid[None, None, :]
    floats = pair_rep.astype(jnp.float32)
    centred = floats - jnp.mean(floats, axis=-1, keepdims=True)
    inv_std = lax.rsqrt(jnp.mean(centred * centred, axis=-1, keepdims=True) + 1e-05)
    unit_rows = centred * inv_std
    normed = (unit_rows * norm_gain).astype(jnp.bfloat16)
    projected = jnp.einsum("ikd,wdc->wick", normed, weights, preferred_element_type=jnp.float32)
    left_side = (pair_valid * jax.nn.sigmoid(projected[1]) * projected[0]).astype(jnp.bfloat16)
    right_side = (pair_valid * jax.nn.sigmoid(projected[3]) * projected[2]).astype(jnp.bfloat16)
    row_panel = lax.all_gather(product_grad, "ja", axis=2, tiled=True)
    panel_part = row_panel
    grad_left = jnp.einsum(
        "icj,jck->ick",
        panel_part,
        lax.all_gather(right_side, "ia", axis=0, tiled=True),
        preferred_element_type=jnp.float32,
    )
    panel_part = row_panel
    grad_right = lax.psum_scatter(
        jnp.einsum("icj,ick->jck", panel_part, left_side, preferred_element_type=jnp.float32),
        "ia",
        scatter_dimension=0,
        tiled=True,
    )
    lin_a, gate_a = gate_terms(grad_left, projected[0], projected[1], pair_valid)
    lin_b, gate_b = gate_terms(grad_right, projected[2], projected[3], pair_valid)
    proj_grads = jnp.stack([lin_a, gate_a, lin_b, gate_b]).astype(jnp.bfloat16)
    grad_part = jnp.einsum("ikd,wick->wdc", normed, proj_grads, preferred_element_type=jnp.float32)
    input_part = jnp.einsum(
        "wick,wdc->ikd", proj_grads, weights, preferred_element_type=jnp.float32
    )
    normed_grad = lax.psum(input_part, "col")
    scaled = normed_grad * norm_gain
    pair_grad = inv_std * (
        scaled
        - jnp.mean(scaled, axis=-1, keepdims=True)
        - unit_rows * jnp.mean(scaled * unit_rows, axis=-1, keepdims=True)
    )
    summed = lax.psum(grad_part, ("ia", "ja"))
    squares = lax.psum(jnp.sum(summed * summed), "col")
    factor = jnp.minimum(1.0, CLIP_LIMIT * lax.rsqrt(squares + 1e-06))
    weight_grads = summed * factor
    return (pair_grad.astype(jnp.bfloat16), weight_grads)


def solution(mesh):
    placed = (P("ia", "ja", None), P(), P(None, None, "col"), P(), P("ia", "col", "ja"))
    return jax.shard_map(
        on_device,
        mesh=mesh,
        in_specs=placed,
        out_specs=(P("ia", "ja", None), P(None, None, "col")),
        check_vma=False,
    )
```

profile of v0, /device:TPU:0, one launch (start us, length us, event | category | flops | bytes accessed | tf_op | source)
XLA Modules:
  0.0 660.3 jit_solution(14896707460684824877)
XLA Ops:
  7.2 4.3 copy.18
  11.5 0.0 all-gather.3.cloned.1.call-start
  11.6 0.1 fusion.41
  11.7 0.1 broadcast_multiply_fusion.1
  11.8 3.5 convert_reduce_fusion
  15.3 4.8 fusion.10
  20.2 4.7 convolution_bitcast_fusion
  24.9 5.9 copy-done.1
  30.8 2.6 multiply_convert_fusion.5
  33.4 0.5 reduce-scatter.2.cloned.1.call-start
  33.9 129.6 %all-gather.5.cloned.1.call-done = bf16[128,64,512]{2,0,1:T(8,128)(2,1)} async-done(((bf16[128,64,128]{2,0,1:T(8,128)(2,1)}), bf16[128,64,512]{2,0,1:T(8,128)(2,1)}) %all-gather.5.cloned.1.call-update) | async-done | bytes 8388624 | tf_op jit(solution)/shard_map/all_gather | solution.py:32
  163.5 87.5 %all-gather.3.cloned.1.call-done = bf16[512,64,128]{2,1,0:T(8,128)(2,1)} async-done(((bf16[128,64,128]{2,1,0:T(8,128)(2,1)}), bf16[512,64,128]{2,1,0:T(8,128)(2,1)}) %all-gather.3.cloned.1.call-update) | async-done | bytes 8388624 | tf_op jit(solution)/shard_map/all_gather | solution.py:37
  251.0 25.2 %fusion.11 = f32[64,128,128]{2,1,0:T(8,128)} fusion(bf16[128,64,512]{2,0,1:T(8,128)(2,1)} %all-gather.5.cloned.1.call-done, bf16[512,64,128]{2,1,0:T(8,128)(2,1)} %all-gather.3.cloned.1.call-done), kind=kOutput, calls=%fused_computation.15 | convolution fusion | flops 1073741824 | bytes 20971520 | tf_op jit(solution)/shard_map/icj,jck->ick/dot_general | solution.py:34
  276.2 5.4 copy.20
  281.6 6.8 %fusion.28 = (bf16[1,128,64,128]{3,2,1,0:T(8,128)(2,1)S(1)}, bf16[1,128,64,128]{3,2,1,0:T(8,128)(2,1)}, bf16[128,64,128]{2,1,0:T(8,128)(2,1)S(1)}) fusion(f32[64,128,128]{1,0,2:T(8,128)} %copy.20, f32[128,128]{1,0:T(8,128)S(1)} %broadcast_multiply_fusion.1, f32[4,128,64,128]{3,2,0,1:T(8,128)} %copy-done.1), kind=kLoop, calls=%fused_computation.43 | loop fusion | flops 14680064 | bytes 18939904 | tf_op jit(solution)/shard_map/stack | solution.py:49
  288.5 14.1 %fusion.32 = f32[64,128,512]{2,1,0:T(8,128)} fusion(bf16[128,64,512]{2,0,1:T(8,128)(2,1)} %all-gather.5.cloned.1.call-done, bf16[128,64,128]{2,1,0:T(8,128)(2,1)S(1)} %get-tuple-element.8), kind=kOutput, calls=%fused_computation.47 | convolution fusion | flops 1073741824 | bytes 27262976 | tf_op jit(solution)/shard_map/icj,ick->jck/dot_general | solution.py:42
  302.6 16.6 %copy.23 = f32[64,128,512]{1,0,2:T(8,128)} copy(f32[64,128,512]{2,1,0:T(8,128)} %fusion.32) | data formatting | bytes 33554432 | tf_op jit(solution)/shard_map/icj,ick->jck/dot_general | solution.py:42
  319.2 0.0 all-reduce.5.cloned.1.call-start
  319.2 153.8 %reduce-scatter.2.cloned.1.call-done = f32[128,64,128]{2,1,0:T(8,128)} async-done(((f32[512,64,128]{2,1,0:T(8,128)}), f32[128,64,128]{2,1,0:T(8,128)}) %reduce-scatter.2.cloned.1.call-update) | async-done | bytes 4194320 | tf_op jit(solution)/shard_map/reduce_scatter | solution.py:41
  473.1 6.0 fusion.30
  479.2 1.3 copy-done.7
  480.4 0.7 copy-done.8
  481.1 5.4 fusion.34
  486.6 0.0 all-reduce.3.cloned.1.call-start
  486.6 6.5 convolution_bitcast_fusion.1
  493.1 99.0 %all-reduce.5.cloned.1.call-done = f32[4,128,64]{1,2,0:T(8,128)} async-done(((f32[4,128,64]{1,2,0:T(8,128)}), f32[4,128,64]{1,2,0:T(8,128)}) %all-reduce.5.cloned.1.call-update) | async-done | bytes 131088 | tf_op jit(solution)/shard_map/psum | solution.py:61
  592.1 1.5 multiply_reduce_fusion.1
  593.7 3.1 psum.23
  597.4 1.6 broadcast_multiply_fusion
  599.0 32.2 %all-reduce.3.cloned.1.call-done = f32[128,128,128]{2,1,0:T(8,128)} async-done(((f32[128,128,128]{2,1,0:T(8,128)}), f32[128,128,128]{2,1,0:T(8,128)}) %all-reduce.3.cloned.1.call-update) | async-done | bytes 8388624 | tf_op jit(solution)/shard_map/psum | solution.py:54
  631.2 11.6 %multiply_reduce_fusion = (f32[128,128]{1,0:T(8,128)S(1)}, f32[128,128]{1,0:T(8,128)S(1)}) fusion(f32[128,128,128]{2,1,0:T(8,128)} %all-reduce.3.cloned.1.call-done, f32[128]{0:T(128)S(1)} %copy-done.9, f32[128,128]{1,0:T(8,128)S(1)} %add_rsqrt_fusion, f32[128,128]{1,0:T(8,128)S(1)} %broadcast_multiply_fusion.4, bf16[128,128,128]{2,1,0:T(8,128)(2,1)} %param.5), kind=kLoop, calls=%fused_computation.17 | loop fusion | flops 14647296 | bytes 12845568 | tf_op jit(solution)/shard_map/reduce_sum | solution.py:58
  642.8 10.7 %fusion.9 = bf16[128,128,128]{2,1,0:T(8,128)(2,1)} fusion(bf16[128,128,128]{2,1,0:T(8,128)(2,1)S(1)} %copy-done.4, f32[128,128,128]{2,1,0:T(8,128)S(1)} %copy-done.5, f32[128,128]{1,0:T(8,128)S(1)} %get-tuple-element.11, f32[128,128]{1,0:T(8,128)S(1)} %get-tuple-element.12, f32[128]{0:T(128)S(1)} %copy-done.9, f32[128,128]{1,0:T(8,128)S(1)} %add_rsqrt_fusion, ...), kind=kLoop, calls=%fused_computation.12 | loop fusion | flops 18874368 | bytes 17039872 | tf_op jit(solution)/shard_map/convert_element_type | solution.py:65
  (29 shorter events, 0.2 us)
Async XLA Ops:
  7.2 13.0 %copy-start = (bf16[4,128,64]{1,2,0:T(8,128)(2,1)S(1)}, bf16[4,128,64]{1,2,0:T(8,128)(2,1)}, u32[]{:S(2)}) copy-start(bf16[4,128,64]{1,2,0:T(8,128)(2,1)} %param.7) | copy-start | bytes 196612
  7.2 4.4 copy-start.10
  7.2 156.3 %all-gather.5.cloned.1.call-start = ((), (), s32[]{:S(2)}) async-start(), calls=%async_computation.2 | async-start | bytes 10485760 | tf_op jit(solution)/shard_map/all_gather | solution.py:32
  11.5 239.5 %all-gather.3.cloned.1.call-start = ((), (), s32[]{:S(2)}) async-start(), calls=%async_computation.1 | async-start | bytes 10485760 | tf_op jit(solution)/shard_map/all_gather | solution.py:37
  11.6 3.7 copy-start.2
  11.8 8.4 %copy-start.9 = (f32[128]{0:T(128)S(1)}, f32[128]{0:T(128)}, u32[]{:S(2)}) copy-start(f32[128]{0:T(128)} %param.6) | copy-start | bytes 1540
  24.9 5.9 copy-start.1
  33.4 439.6 %reduce-scatter.2.cloned.1.call-start = ((), (), s32[]{:S(2)}) async-start(), calls=%async_computation.3 | async-start | bytes 20971520 | tf_op jit(solution)/shard_map/reduce_scatter | solution.py:41
  319.2 272.9 %all-reduce.5.cloned.1.call-start = ((), (), s32[]{:S(2)}) async-start(), calls=%async_computation.5 | async-start | bytes 262144 | tf_op jit(solution)/shard_map/psum | solution.py:61
  473.1 8.0 %copy-start.3 = (bf16[128,128,128]{2,1,0:T(8,128)(2,1)S(1)}, bf16[128,128,128]{2,1,0:T(8,128)(2,1)}, u32[]{:S(2)}) copy-start(bf16[128,128,128]{2,1,0:T(8,128)(2,1)} %param.5) | copy-start | bytes 12582916
  473.1 8.0 %copy-start.6 = (bf16[1,128,64,128]{3,2,1,0:T(8,128)(2,1)S(1)}, bf16[1,128,64,128]{3,2,1,0:T(8,128)(2,1)}, u32[]{:S(2)}) copy-start(bf16[1,128,64,128]{3,2,1,0:T(8,128)(2,1)} %get-tuple-element.5) | copy-start | bytes 6291460
  479.1 1.3 copy-start.7
  479.1 2.0 copy-start.8
  486.6 144.6 %all-reduce.3.cloned.1.call-start = ((), (), s32[]{:S(2)}) async-start(), calls=%async_computation.4 | async-start | bytes 16777216 | tf_op jit(solution)/shard_map/psum | solution.py:54
  631.2 11.6 %copy-start.4 = (bf16[128,128,128]{2,1,0:T(8,128)(2,1)S(1)}, bf16[128,128,128]{2,1,0:T(8,128)(2,1)}, u32[]{:S(2)}) copy-start(bf16[128,128,128]{2,1,0:T(8,128)(2,1)} %param.5) | copy-start | bytes 12582916
  631.2 11.6 %copy-start.5 = (f32[128,128,128]{2,1,0:T(8,128)S(1)}, f32[128,128,128]{2,1,0:T(8,128)}, u32[]{:S(2)}) copy-start(f32[128,128,128]{2,1,0:T(8,128)} %all-reduce.3.cloned.1.call-done) | copy-start | bytes 25165828
Sparse Core Ops, SparseCore 0:
  11.6 151.8 all-gather.4
  165.4 85.6 all-gather.2
  319.3 153.7 reduce-scatter.1
  486.7 105.3 all-reduce.4
  594.4 36.6 all-reduce.2
where the time goes:
time: 668 us; the launch traced here: 660 us
  waiting for transfers between devices  502 us (75%)
  matrix products  55.9 us (8%)
  other arithmetic  49.3 us (7%)
  local copies, waits for them, and re-layouts  34.2 us (5%)
  between operations  14.9 us (2%)
    reduce_scatter x1, waiting for transfers between devices, on_device(): lax.psum_scatter(jnp.einsum('icj,ick->jck', panel_part, left_side, prefer...  154 us
    all_gather x1, waiting for transfers between devices, on_device(): row_panel = lax.all_gather(product_grad, 'ja', axis=2, tiled=True)  130 us
    psum x1, waiting for transfers between devices, on_device(): summed = lax.psum(grad_part, ('ia', 'ja'))  99 us
    all_gather x1, waiting for transfers between devices, on_device(): lax.all_gather(right_side, 'ia', axis=0, tiled=True)  87.5 us
    psum x1, waiting for transfers between devices, on_device(): normed_grad = lax.psum(input_part, 'col')  32.2 us
    dot_general x1, matrix products, on_device(): jnp.einsum('icj,jck->ick', panel_part, lax.all_gather(right_side, 'ia', a...  25.2 us
    dot_general x1, local copies, waits for them, and re-layouts, on_device(): jnp.einsum('icj,ick->jck', panel_part, left_side, preferred_element_type=...  16.6 us
    dot_general x1, matrix products, on_device(): jnp.einsum('icj,ick->jck', panel_part, left_side, preferred_element_type=...  14.1 us
  transfers between devices with their start and end apart: 5, of which 5 were waited for; matrix products, arithmetic and copies ran while one was open for 4% of the time, Pallas kernels for 0%

commit v1 on v0

--- a/solution.py
+++ b/solution.py
@@ -58,7 +58,8 @@
         - jnp.mean(scaled, axis=-1, keepdims=True)
         - unit_rows * jnp.mean(scaled * unit_rows, axis=-1, keepdims=True)
     )
-    summed = lax.psum(grad_part, ("ia", "ja"))
+    _reach_face = lambda mat: lax.psum(lax.psum(mat, axis_name="ja"), axis_name="ia")
+    summed = _reach_face(grad_part)
     squares = lax.psum(jnp.sum(summed * summed), "col")
     factor = jnp.minimum(1.0, CLIP_LIMIT * lax.rsqrt(squares + 1e-06))
     weight_grads = summed * factor

time: 668 us -> 643 us (0.963)
  waiting for transfers between devices: 502 us -> 477 us
    psum x1 -> x2, waiting for transfers between devices: 99 us -> 72.8 us  [the longest x1 38.1 us: on_device(): lax.psum(lax.psum(mat, axis_name='ja'), axis_name='ia')]
  transfers between devices with their start and end apart: 5 -> 6, of which waited for: 5 -> 6; matrix products, arithmetic and copies ran while one was open for 4% -> 4% of each run, Pallas kernels for 0% -> 0%
where the time goes in v1:
time: 643 us; the launch traced here: 635 us
  waiting for transfers between devices  477 us (74%)
  matrix products  55.9 us (9%)
  other arithmetic  49.3 us (8%)
  local copies, waits for them, and re-layouts  34.2 us (5%)
  between operations  15.2 us (2%)
    reduce_scatter x1, waiting for transfers between devices, on_device(): lax.psum_scatter(jnp.einsum('icj,ick->jck', panel_part, left_side, prefer...  154 us
    all_gather x1, waiting for transfers between devices, on_device(): row_panel = lax.all_gather(product_grad, 'ja', axis=2, tiled=True)  130 us
    all_gather x1, waiting for transfers between devices, on_device(): lax.all_gather(right_side, 'ia', axis=0, tiled=True)  87.5 us
    psum x1, waiting for transfers between devices, on_device(): lax.psum(lax.psum(mat, axis_name='ja'), axis_name='ia')  38.1 us
    psum x1, waiting for transfers between devices, on_device(): lax.psum(mat, axis_name='ja')  34.7 us
    psum x1, waiting for transfers between devices, on_device(): normed_grad = lax.psum(input_part, 'col')  33.1 us
    dot_general x1, matrix products, on_device(): jnp.einsum('icj,jck->ick', panel_part, lax.all_gather(right_side, 'ia', a...  25.2 us
    dot_general x1, local copies, waits for them, and re-layouts, on_device(): jnp.einsum('icj,ick->jck', panel_part, left_side, preferred_element_type=...  16.6 us
  transfers between devices with their start and end apart: 6, of which 6 were waited for; matrix products, arithmetic and copies ran while one was open for 4% of the time, Pallas kernels for 0%

profile of v1, /device:TPU:0, one launch (start us, length us, event | category | flops | bytes accessed | tf_op | source)
XLA Modules:
  0.0 635.5 jit_solution(1944610599505219290)
XLA Ops:
  7.2 4.3 copy.18
  11.5 0.0 all-gather.3.cloned.1.call-start
  11.6 0.1 fusion.41
  11.7 0.1 broadcast_multiply_fusion.1
  11.8 3.5 convert_reduce_fusion
  15.3 4.8 fusion.10
  20.2 4.7 convolution_bitcast_fusion
  24.9 5.9 copy-done.1
  30.8 2.6 multiply_convert_fusion.5
  33.4 0.5 reduce-scatter.2.cloned.1.call-start
  33.9 129.6 %all-gather.5.cloned.1.call-done = bf16[128,64,512]{2,0,1:T(8,128)(2,1)} async-done(((bf16[128,64,128]{2,0,1:T(8,128)(2,1)}), bf16[128,64,512]{2,0,1:T(8,128)(2,1)}) %all-gather.5.cloned.1.call-update) | async-done | bytes 8388624 | tf_op jit(solution)/shard_map/all_gather | solution.py:32
  163.5 87.5 %all-gather.3.cloned.1.call-done = bf16[512,64,128]{2,1,0:T(8,128)(2,1)} async-done(((bf16[128,64,128]{2,1,0:T(8,128)(2,1)}), bf16[512,64,128]{2,1,0:T(8,128)(2,1)}) %all-gather.3.cloned.1.call-update) | async-done | bytes 8388624 | tf_op jit(solution)/shard_map/all_gather | solution.py:37
  251.0 25.2 %fusion.11 = f32[64,128,128]{2,1,0:T(8,128)} fusion(bf16[128,64,512]{2,0,1:T(8,128)(2,1)} %all-gather.5.cloned.1.call-done, bf16[512,64,128]{2,1,0:T(8,128)(2,1)} %all-gather.3.cloned.1.call-done), kind=kOutput, calls=%fused_computation.15 | convolution fusion | flops 1073741824 | bytes 20971520 | tf_op jit(solution)/shard_map/icj,jck->ick/dot_general | solution.py:34
  276.2 5.4 copy.20
  281.6 6.8 %fusion.28 = (bf16[1,128,64,128]{3,2,1,0:T(8,128)(2,1)S(1)}, bf16[1,128,64,128]{3,2,1,0:T(8,128)(2,1)}, bf16[128,64,128]{2,1,0:T(8,128)(2,1)S(1)}) fusion(f32[64,128,128]{1,0,2:T(8,128)} %copy.20, f32[128,128]{1,0:T(8,128)S(1)} %broadcast_multiply_fusion.1, f32[4,128,64,128]{3,2,0,1:T(8,128)} %copy-done.1), kind=kLoop, calls=%fused_computation.43 | loop fusion | flops 14680064 | bytes 18939904 | tf_op jit(solution)/shard_map/stack | solution.py:49
  288.5 14.1 %fusion.32 = f32[64,128,512]{2,1,0:T(8,128)} fusion(bf16[128,64,512]{2,0,1:T(8,128)(2,1)} %all-gather.5.cloned.1.call-done, bf16[128,64,128]{2,1,0:T(8,128)(2,1)S(1)} %get-tuple-element.8), kind=kOutput, calls=%fused_computation.47 | convolution fusion | flops 1073741824 | bytes 27262976 | tf_op jit(solution)/shard_map/icj,ick->jck/dot_general | solution.py:42
  302.6 16.6 %copy.23 = f32[64,128,512]{1,0,2:T(8,128)} copy(f32[64,128,512]{2,1,0:T(8,128)} %fusion.32) | data formatting | bytes 33554432 | tf_op jit(solution)/shard_map/icj,ick->jck/dot_general | solution.py:42
  319.2 0.0 all-reduce.6.cloned.1.call-start
  319.2 153.8 %reduce-scatter.2.cloned.1.call-done = f32[128,64,128]{2,1,0:T(8,128)} async-done(((f32[512,64,128]{2,1,0:T(8,128)}), f32[128,64,128]{2,1,0:T(8,128)}) %reduce-scatter.2.cloned.1.call-update) | async-done | bytes 4194320 | tf_op jit(solution)/shard_map/reduce_scatter | solution.py:41
  473.1 6.0 fusion.30
  479.2 1.3 copy-done.7
  480.4 0.7 copy-done.8
  481.1 5.4 fusion.34
  486.6 34.7 %all-reduce.6.cloned.1.call-done = f32[4,128,64]{1,2,0:T(8,128)} async-done(((f32[4,128,64]{1,2,0:T(8,128)}), f32[4,128,64]{1,2,0:T(8,128)}) %all-reduce.6.cloned.1.call-update) | async-done | bytes 131088 | tf_op jit(solution)/shard_map/psum | solution.py:61
  521.4 6.5 %convolution_bitcast_fusion.1 = f32[128,128,128]{2,1,0:T(8,128)} fusion(bf16[1,128,64,128]{3,2,1,0:T(8,128)(2,1)} %copy-done.8, bf16[1,128,64,128]{3,2,1,0:T(8,128)(2,1)} %copy-done.7, bf16[1,128,64,128]{3,2,1,0:T(8,128)(2,1)} %get-tuple-element.5, bf16[1,128,64,128]{3,2,1,0:T(8,128)(2,1)S(1)} %get-tuple-element.4, bf16[4,128,64]{1,2,0:T(8,128)(2,1)S(1)} %copy-done), kind=kOutput, calls=%fused_computation.42 | convolution fusion | flops 1086324736 | bytes 16842752 | tf_op jit(solution)/shard_map/wick,wdc->ikd/dot_general | solution.py:51
  527.9 38.1 %all-reduce.8.cloned.1.call-done = f32[4,128,64]{1,2,0:T(8,128)} async-done(((f32[4,128,64]{1,2,0:T(8,128)}), f32[4,128,64]{1,2,0:T(8,128)}) %all-reduce.8.cloned.1.call-update) | async-done | bytes 131088 | tf_op jit(solution)/shard_map/psum | solution.py:61
  566.0 1.5 multiply_reduce_fusion.1
  567.5 3.1 psum.31
  571.3 1.6 broadcast_multiply_fusion
  572.9 33.1 %all-reduce.4.cloned.1.call-done = f32[128,128,128]{2,1,0:T(8,128)} async-done(((f32[128,128,128]{2,1,0:T(8,128)}), f32[128,128,128]{2,1,0:T(8,128)}) %all-reduce.4.cloned.1.call-update) | async-done | bytes 8388624 | tf_op jit(solution)/shard_map/psum | solution.py:54
  606.0 11.6 %multiply_reduce_fusion = (f32[128,128]{1,0:T(8,128)S(1)}, f32[128,128]{1,0:T(8,128)S(1)}) fusion(f32[128,128,128]{2,1,0:T(8,128)} %all-reduce.4.cloned.1.call-done, f32[128]{0:T(128)S(1)} %copy-done.9, f32[128,128]{1,0:T(8,128)S(1)} %add_rsqrt_fusion, f32[128,128]{1,0:T(8,128)S(1)} %broadcast_multiply_fusion.4, bf16[128,128,128]{2,1,0:T(8,128)(2,1)} %param.5), kind=kLoop, calls=%fused_computation.17 | loop fusion | flops 14647296 | bytes 12845568 | tf_op jit(solution)/shard_map/reduce_sum | solution.py:58
  617.7 10.7 %fusion.9 = bf16[128,128,128]{2,1,0:T(8,128)(2,1)} fusion(bf16[128,128,128]{2,1,0:T(8,128)(2,1)S(1)} %copy-done.4, f32[128,128,128]{2,1,0:T(8,128)S(1)} %copy-done.5, f32[128,128]{1,0:T(8,128)S(1)} %get-tuple-element.11, f32[128,128]{1,0:T(8,128)S(1)} %get-tuple-element.12, f32[128]{0:T(128)S(1)} %copy-done.9, f32[128,128]{1,0:T(8,128)S(1)} %add_rsqrt_fusion, ...), kind=kLoop, calls=%fused_computation.12 | loop fusion | flops 18874368 | bytes 17039872 | tf_op jit(solution)/shard_map/convert_element_type | solution.py:66
  (32 shorter events, 0.3 us)
Async XLA Ops:
  7.2 13.0 %copy-start = (bf16[4,128,64]{1,2,0:T(8,128)(2,1)S(1)}, bf16[4,128,64]{1,2,0:T(8,128)(2,1)}, u32[]{:S(2)}) copy-start(bf16[4,128,64]{1,2,0:T(8,128)(2,1)} %param.7) | copy-start | bytes 196612
  7.2 4.4 copy-start.10
  7.2 156.3 %all-gather.5.cloned.1.call-start = ((), (), s32[]{:S(2)}) async-start(), calls=%async_computation.2 | async-start | bytes 10485760 | tf_op jit(solution)/shard_map/all_gather | solution.py:32
  11.5 239.5 %all-gather.3.cloned.1.call-start = ((), (), s32[]{:S(2)}) async-start(), calls=%async_computation.1 | async-start | bytes 10485760 | tf_op jit(solution)/shard_map/all_gather | solution.py:37
  11.6 3.7 copy-start.2
  11.8 8.4 %copy-start.9 = (f32[128]{0:T(128)S(1)}, f32[128]{0:T(128)}, u32[]{:S(2)}) copy-start(f32[128]{0:T(128)} %param.6) | copy-start | bytes 1540
  24.9 5.9 copy-start.1
  33.4 439.6 %reduce-scatter.2.cloned.1.call-start = ((), (), s32[]{:S(2)}) async-start(), calls=%async_computation.3 | async-start | bytes 20971520 | tf_op jit(solution)/shard_map/reduce_scatter | solution.py:41
  319.2 202.1 %all-reduce.6.cloned.1.call-start = ((), (), s32[]{:S(2)}) async-start(), calls=%async_computation.5 | async-start | bytes 262144 | tf_op jit(solution)/shard_map/psum | solution.py:61
  473.1 8.0 %copy-start.3 = (bf16[128,128,128]{2,1,0:T(8,128)(2,1)S(1)}, bf16[128,128,128]{2,1,0:T(8,128)(2,1)}, u32[]{:S(2)}) copy-start(bf16[128,128,128]{2,1,0:T(8,128)(2,1)} %param.5) | copy-start | bytes 12582916
  473.1 8.0 %copy-start.6 = (bf16[1,128,64,128]{3,2,1,0:T(8,128)(2,1)S(1)}, bf16[1,128,64,128]{3,2,1,0:T(8,128)(2,1)}, u32[]{:S(2)}) copy-start(bf16[1,128,64,128]{3,2,1,0:T(8,128)(2,1)} %get-tuple-element.5) | copy-start | bytes 6291460
  479.1 1.3 copy-start.7
  479.1 2.0 copy-start.8
  486.6 79.4 %all-reduce.8.cloned.1.call-start = ((), (), s32[]{:S(2)}) async-start(), calls=%async_computation.6 | async-start | bytes 262144 | tf_op jit(solution)/shard_map/psum | solution.py:61
  521.4 84.6 %all-reduce.4.cloned.1.call-start = ((), (), s32[]{:S(2)}) async-start(), calls=%async_computation.4 | async-start | bytes 16777216 | tf_op jit(solution)/shard_map/psum | solution.py:54
  606.0 11.6 %copy-start.4 = (bf16[128,128,128]{2,1,0:T(8,128)(2,1)S(1)}, bf16[128,128,128]{2,1,0:T(8,128)(2,1)}, u32[]{:S(2)}) copy-start(bf16[128,128,128]{2,1,0:T(8,128)(2,1)} %param.5) | copy-start | bytes 12582916
  606.0 11.6 %copy-start.5 = (f32[128,128,128]{2,1,0:T(8,128)S(1)}, f32[128,128,128]{2,1,0:T(8,128)}, u32[]{:S(2)}) copy-start(f32[128,128,128]{2,1,0:T(8,128)} %all-reduce.4.cloned.1.call-done) | copy-start | bytes 25165828
Sparse Core Ops, SparseCore 0:
  11.6 151.8 all-gather.4
  165.4 85.6 all-gather.2
  319.3 153.7 reduce-scatter.1
  486.7 34.6 all-reduce.5
  524.1 41.8 all-reduce.7
  568.3 37.6 all-reduce.3
